TPU v7x, 32 devices: a whole 2x2x4 slice. The times are simulated.
32 devices in a mesh: heads: 2 (over x), tokens: 16 (over z, y, core).
Axes of the slice: x: 2, y: 2, z: 4, core: 2. Of those that a mesh axis runs over, the one named last changes fastest.
Arguments:
- queries: bfloat16 [128, 16, 576], P('heads', 'tokens'), may hold values from -40 to 40
- latent_keys: bfloat16 [16384, 576], P('tokens'), may hold values from -4 to 4
- index_queries: bfloat16 [16, 64, 128], P(None, 'heads'), may hold values from -4 to 4
- index_keys: bfloat16 [16384, 128], P('tokens'), may hold values from -8 to 8
- index_weights: float32 [16, 64], P(None, 'heads'), may hold values from 0 to 1.2
- positions: int32 [16], replicated, may hold values from 8192 to 16383
Outputs:
- index_query_grad: float32 [16, 64, 128], P(None, 'heads')
- index_weight_grad: float32 [16, 64], P(None, 'heads')
- index_key_grad: float32 [16384, 128], P('tokens')
All inputs are finite; a program needn't handle non-finite values.
Results may differ from a plain program's by a relative error of at most 0.0026.
Values may be sent and summed in bfloat16 or wider, within the bound.
A program may use at most 64 MiB of HBM per device.

v0:
```python
import jax
import jax.numpy as jnp
from jax import lax
from jax.sharding import PartitionSpec as P

H = 128


softmax_scale = 192.0 ** (-0.5)
masked_value = -1e30


def merged(value, axis, combine):
    everything = jax.tree.map(lambda part: lax.all_gather(part, axis), value)
    first = jax.tree.map(lambda part: part[0], everything)

    def lap(k, so_far):
        return combine(so_far, jax.tree.map(lambda part: part[k], everything))

    return lax.fori_loop(1, lax.axis_size(axis), lap, first)


def block_size(heads_here, row_limit):
    chosen = 1
    for option in range(1, heads_here + 1):
        if heads_here % option == 0 and option <= row_limit:
            chosen = option
    return chosen


def joined_stats(first_pair, second_pair):
    maximum = jnp.maximum(first_pair[0], second_pair[0])
    totals = first_pair[1] * jnp.exp(first_pair[0] - maximum) + second_pair[1] * jnp.exp(
        second_pair[0] - maximum
    )
    return (maximum, totals)


def global_stats(local_max, local_total):
    maximum, totals = merged((local_max, local_total), "tokens", joined_stats)
    return (maximum, totals)


def logit_grad(summed_target, logits, visible, loss_scale):
    target = summed_target / H
    masked = jnp.where(visible, logits, masked_value)
    local_max = jnp.max(masked, axis=1)
    local_total = jnp.sum(jnp.exp(masked - local_max[:, None]), axis=1)
    maximum, totals = global_stats(local_max, local_total)
    index_probs = jnp.exp(masked - maximum[:, None]) / totals[:, None]
    return loss_scale * (index_probs - target)


def local(queries, latent_keys, index_queries, index_keys, index_weights, positions):
    key_count = latent_keys.shape[0]
    loss_scale = key_count * lax.axis_size("tokens") // 8
    offset = lax.axis_index("tokens") * key_count
    key_index = offset + jnp.arange(key_count, dtype=jnp.int32)
    visible = key_index[None, :] <= positions[:, None]
    gathered = lax.all_gather(queries, "tokens", axis=1, tiled=True)
    head_count, query_count, width_qk = gathered.shape
    per_block = block_size(head_count, max(1, 512 // query_count))
    head_blocks = gathered.reshape(head_count // per_block, per_block, query_count, width_qk)

    def block_scores(head_block):
        scores = (
            jnp.einsum("hqd,kd->hqk", head_block, latent_keys, preferred_element_type=jnp.float32)
            * softmax_scale
        )
        return jnp.where(visible[None], scores, masked_value)

    def block_stats(head_block):
        scores = block_scores(head_block)
        maximum = jnp.max(scores, axis=2)
        return (maximum, jnp.sum(jnp.exp(scores - maximum[..., None]), axis=2))

    local_max, local_total = lax.map(block_stats, head_blocks)
    head_max, head_total = global_stats(local_max, local_total)

    def accumulate(running, inputs):
        head_block, maximum, totals = inputs
        scores = block_scores(head_block)
        probabilities = jnp.exp(scores - maximum[..., None]) / totals[..., None]
        return (running + jnp.sum(probabilities, axis=0), None)

    partial_target, _ = lax.scan(
        accumulate,
        jnp.zeros((query_count, key_count), jnp.float32),
        (head_blocks, head_max, head_total),
    )
    index_scale = index_queries.shape[2] ** (-0.5)
    active = (
        jnp.einsum("qjd,kd->qjk", index_queries, index_keys, preferred_element_type=jnp.float32)
        * index_scale
    )
    rectified = jnp.maximum(active, 0.0)
    partial_logits = jnp.sum(index_weights[:, :, None] * rectified, axis=1)
    full_target, full_logits = lax.psum((partial_target, partial_logits), "heads")
    dlogit = logit_grad(full_target, full_logits, visible, loss_scale)
    gate_grad = (dlogit[:, None, :] * index_weights[:, :, None] * (active > 0.0)).astype(
        jnp.bfloat16
    )
    query_local = (
        jnp.einsum("qjk,kd->qjd", gate_grad, index_keys, preferred_element_type=jnp.float32)
        * index_scale
    )
    weight_local = jnp.sum(dlogit[:, None, :] * rectified, axis=2)
    query_grad, weight_grad = lax.psum((query_local, weight_local), "tokens")
    key_local = (
        jnp.einsum("qjk,qjd->kd", gate_grad, index_queries, preferred_element_type=jnp.float32)
        * index_scale
    )
    key_grad = lax.psum(key_local, "heads")
    return (query_grad, weight_grad, key_grad)


def solution(mesh):
    placed = (
        P("heads", "tokens", None),
        P("tokens", None),
        P(None, "heads", None),
        P("tokens", None),
        P(None, "heads"),
        P(),
    )
    return jax.shard_map(
        local,
        mesh=mesh,
        in_specs=placed,
        out_specs=(P(None, "heads", None), P(None, "heads"), P("tokens", None)),
        check_vma=False,
    )
```

profile of v0, /device:TPU:0, one launch (start us, length us, event | category | flops | bytes accessed | tf_op | source)
XLA Modules:
  0.0 293.5 jit_solution(14226321482201885906)
XLA Ops:
  7.2 0.7 all-gather.6.cloned.1.call-update
  8.0 1.2 dynamic-slice
  9.9 2.1 multiply_reduce_fusion.1
  12.0 39.6 %all-gather.6.cloned.1.call-done = bf16[64,16,576]{2,0,1:T(8,128)(2,1)} async-done(((bf16[64,1,576]{2,0,1:T(8,128)(2,1)}), bf16[64,16,576]{2,0,1:T(8,128)(2,1)}) %all-gather.6.cloned.1.call-update) | async-done | bytes 1179664 | tf_op jit(solution)/shard_map/all_gather | solution.py:60
  51.6 3.1 %copy.18 = bf16[2,32,16,576]{3,2,1,0:T(8,128)(2,1)} copy(bf16[2,32,16,576]{3,1,0,2:T(8,128)(2,1)} %bitcast.83) | data formatting | bytes 2359296
  54.8 6.8 %while.60 = (s32[]{:T(128)}, f32[2,32,16]{1,2,0:T(8,128)S(1)}, f32[2,32,16]{1,2,0:T(8,128)S(1)}, bf16[2,32,16,576]{3,2,1,0:T(8,128)(2,1)}, bf16[1024,576]{0,1:T(...) while((s32[]{:T(128)}, f32[2,32,16]{1,2,0:T(8,128)S(1)}, ...), condition=%wide.region_9.10_spmd.clone, body=%wide.region_6.9_spmd.clone.sunk | while | flops 607665152 | bytes 6130329 | solution.py:77
  54.8 0.1 broadcast_compare_fusion.4
  54.9 2.6 fusion.49
  57.4 0.6 exponential_reduce_fusion.3
  58.0 0.1 copy.34
  58.1 0.1 copy.35
  58.1 0.1 broadcast_compare_fusion.4
  58.2 2.6 fusion.49
  60.8 0.6 exponential_reduce_fusion.3
  61.4 0.1 copy.34
  61.5 0.1 copy.35
  61.5 19.9 %all-gather.2 = f32[32,32,16]{1,2,0:T(8,128)S(1)} all-gather(f32[2,32,16]{1,2,0:T(8,128)S(1)} %get-tuple-element.341), channel_id=4, replica_groups=mesh['heads'=2,'tokens'=16] {'tokens'}, dimensions={0}, use_global_device_ids=true | all-gather | bytes 69632 | tf_op jit(solution)/shard_map/all_gather | solution.py:14
  81.4 18.1 %all-gather.3 = f32[32,32,16]{1,2,0:T(8,128)S(1)} all-gather(f32[2,32,16]{1,2,0:T(8,128)S(1)} %get-tuple-element.342), channel_id=5, replica_groups=mesh['heads'=2,'tokens'=16] {'tokens'}, dimensions={0}, use_global_device_ids=true | all-gather | bytes 69632 | tf_op jit(solution)/shard_map/all_gather | solution.py:14
  99.6 0.7 while.59
  100.3 6.0 %while.61 = (s32[]{:T(128)}, f32[16,1024]{1,0:T(8,128)S(1)}, bf16[2,32,16,576]{3,2,1,0:T(8,128)(2,1)}, bf16[1024,576]{0,1:T(8,128)(2,1)}, f32[2,32,16]{1,2,0:T(8...) while((s32[]{:T(128)}, f32[16,1024]{1,0:T(8,128)S(1)}, ...), condition=%wide.region_14.15_spmd.clone, body=%wide.region_12.14_spmd.clone.sunk | while | flops 606633984 | bytes 2155187 | solution.py:86
  100.3 0.1 copy.36
  100.4 0.1 copy.37
  100.5 0.1 broadcast_compare_fusion.5
  100.5 2.7 fusion.52
  103.3 0.1 copy.36
  103.4 0.1 copy.37
  103.5 0.1 broadcast_compare_fusion.5
  103.5 2.7 fusion.52
  106.3 0.6 copy-done.1
  107.0 0.3 fusion.20
  107.3 19.7 %all-reduce.12.cloned.1.call-done = (f32[16,1024]{1,0:T(8,128)}, f32[16,1024]{1,0:T(8,128)}) async-done(((f32[16,1024]{1,0:T(8,128)}, f32[16,1024]{1,0:T(8,128)}), (f32[16,1024]{1,0:T(8,128)}, f32[16,1024]{1,0:T(8,128)})) %all-reduce.12.cloned.1.call-update) | async-done | bytes 131088 | tf_op jit(solution)/shard_map/psum | solution.py:98
  127.1 1.0 fusion.34
  128.1 1.0 exponential_reduce_fusion.1
  129.1 0.2 dynamic-update-slice
  129.4 0.2 dynamic-update-slice.1
  129.6 32.6 %all-reduce.2 = (f32[256]{0:T(256)S(1)}, f32[256]{0:T(256)S(1)}) all-reduce(f32[256]{0:T(256)S(1)} %dynamic-update-slice, f32[256]{0:T(256)S(1)} %dynamic-update-slice.1), channel_id=2, replica_groups=mesh['heads'=2,'tokens'=16] {'tokens'}, use_global_device_ids=true, to_apply=%add | all-reduce | flops 512 | bytes 4096
  162.2 0.1 reshape.27
  162.3 0.1 reshape.28
  162.4 0.7 while.58
  163.1 1.0 subtract_multiply_fusion
  164.1 1.2 convolution_multiply_fusion
  165.3 1.4 fusion.19
  166.8 0.4 multiply_reduce_fusion
  167.2 30.6 %psum.38 = f32[16,32]{1,0:T(8,128)} all-reduce(f32[16,32]{1,0:T(8,128)S(1)} %multiply_reduce_fusion), channel_id=1, replica_groups=mesh['heads'=2,'tokens'=16] {'tokens'}, use_global_device_ids=true, to_apply=%region_18.19 | all-reduce | flops 512 | bytes 4096 | tf_op jit(solution)/shard_map/psum | solution.py:108
  197.8 53.7 %all-reduce.8.cloned.1.call-done = f32[16,32,128]{2,1,0:T(8,128)} async-done(((f32[16,32,128]{2,1,0:T(8,128)}), f32[16,32,128]{2,1,0:T(8,128)}) %all-reduce.8.cloned.1.call-update) | async-done | bytes 262160 | tf_op jit(solution)/shard_map/psum | solution.py:108
  251.5 31.9 %all-reduce.10.cloned.1.call-done = f32[1024,128]{1,0:T(8,128)} async-done(((f32[1024,128]{1,0:T(8,128)}), f32[1024,128]{1,0:T(8,128)}) %all-reduce.10.cloned.1.call-update) | async-done | bytes 524304 | tf_op jit(solution)/shard_map/psum | solution.py:113
  283.4 1.7 copy.79
  285.1 1.9 copy.80
  (62 shorter events, 1.1 us)
Async XLA Ops:
  7.2 2.7 copy-start
  7.2 44.5 %all-gather.6.cloned.1.call-start = ((), (), s32[]{:S(2)}) async-start(), calls=%async_computation | async-start | bytes 1392640 | tf_op jit(solution)/shard_map/all_gather | solution.py:60
  7.9 119.1 %all-reduce.12.cloned.1.call-start = ((), (), s32[]{:S(2)}) async-start(), calls=%async_computation.3 | async-start | bytes 262144 | tf_op jit(solution)/shard_map/psum | solution.py:98
  9.9 44.9 %copy-start.3 = (s32[16]{0:T(128)S(1)}, s32[16]{0:T(128)}, u32[]{:S(2)}) copy-start(s32[16]{0:T(128)} %param.19) | copy-start | bytes 196
  106.3 0.6 copy-start.1
  106.3 57.7 %copy-start.4 = (f32[16,32]{1,0:T(8,128)S(1)}, f32[16,32]{1,0:T(8,128)}, u32[]{:S(2)}) copy-start(f32[16,32]{1,0:T(8,128)} %param.18) | copy-start | bytes 6148
  107.0 144.6 %all-reduce.8.cloned.1.call-start = ((), (), s32[]{:S(2)}) async-start(), calls=%async_computation.1 | async-start | bytes 524288 | tf_op jit(solution)/shard_map/psum | solution.py:108
  164.0 1.3 copy-start.2
  165.3 118.1 %all-reduce.10.cloned.1.call-start = ((), (), s32[]{:S(2)}) async-start(), calls=%async_computation.2 | async-start | bytes 1048576 | tf_op jit(solution)/shard_map/psum | solution.py:113
Sparse Core Ops, SparseCore 0:
  10.3 41.3 all-gather.5
  107.1 19.9 all-reduce.11
  165.4 86.0 all-reduce.7
  254.3 29.1 all-reduce.9
where the time goes:
time: 294 us; the launch traced here: 293 us
  waiting for transfers between devices  146 us (50%)
  blocking collectives  101 us (34%)
  matrix products  15.3 us (5%)
  between operations  14.6 us (5%)
  local copies, waits for them, and re-layouts  9.76 us (3%)
  other arithmetic  6 us (2%)
    psum x1, waiting for transfers between devices, local(): query_grad, weight_grad = lax.psum((query_local, weight_local), 'tokens')  53.7 us
    all_gather x1, waiting for transfers between devices, local(): gathered = lax.all_gather(queries, 'tokens', axis=1, tiled=True)  39.6 us
    all_gather x2, blocking collectives, merged(): everything = jax.tree.map(lambda part: lax.all_gather(part, axis), value)  38 us
    unnamed x1, blocking collectives  32.6 us
    psum x1, waiting for transfers between devices, local(): key_grad = lax.psum(key_local, 'heads')  31.9 us
    psum x1, blocking collectives, local(): query_grad, weight_grad = lax.psum((query_local, weight_local), 'tokens')  30.6 us
    psum x1, waiting for transfers between devices, local(): lax.psum((partial_target, partial_logits), 'heads')  19.7 us
    dot_general x4, matrix products, block_scores(): jnp.einsum('hqd,kd->hqk', head_block, latent_keys, preferred_element_type...  10.6 us
  transfers between devices with their start and end apart: 4, of which 4 were waited for; matrix products, arithmetic and copies ran while one was open for 2% of the time, Pallas kernels for 0%

commit v1 on v0

v1 whole, which is shorter than its diff:
```python
import functools

import jax
import jax.numpy as jnp
from jax import lax
from jax.experimental import pallas as pl
from jax.experimental.pallas import tpu as pltpu
from jax.sharding import PartitionSpec as P

MESH = pl.DeviceIdType.MESH
softmax_scale = 192.0 ** (-0.5)
masked_value = -1e30
open_value = 3e38
f32 = jnp.float32
bf16 = jnp.bfloat16


def swapped(value, step, size):
    if size & (size - 1):
        return lax.rem(value + step, size)
    out = value
    bit = 1
    while bit < size:
        if step & bit:
            out = out + bit - 2 * bit * lax.rem(lax.div(value, bit), 2)
        bit *= 2
    return out


def as_row(column, eye):
    return jnp.sum(jnp.where(eye, column, 0.0), axis=0, keepdims=True)


def eye_of(rows):
    return lax.broadcasted_iota(jnp.int32, (rows, 128), 0) == lax.broadcasted_iota(jnp.int32, (rows, 128), 1)


def kernel(
    cfg, q_in, k_in, iq_in, ik_in, w_in, pos_ref, qg_out, kg_out,
    qbuf, kbuf, iqbuf, ikbuf, wbuf, wcol, p, act, gate, ml, mrow, colm, coll, stats, istats, tbuf, dbuf,
    qpart, pairbuf, rsend, rsbuf, agbuf,
    lsem, zs, ys, cs, qr, hs, hr, ws, wr, ss, sr, iss, isr, ts, tr, ps, pr, rs, rr, gs, gr,
):
    NH, N, Z, Y, Q, R, D, Kl, Jl, SL, H, loss_scale = cfg
    G = 2 * Y
    NC = N // 2
    me = lax.axis_index("tokens")
    mh = lax.axis_index("heads")
    core = lax.rem(me, 2)
    chip = lax.div(me, 2)
    y = lax.rem(chip, Y)
    z = lax.div(chip, Y)
    partner = me + 1 - 2 * core

    def at(zz, yy, cc):
        return (zz * Y + yy) * 2 + cc

    def remote(src, dst, send, recv, tok=None, head=None):
        device = {"tokens": tok} if head is None else {"heads": head}
        return pltpu.make_async_remote_copy(
            src_ref=src, dst_ref=dst, send_sem=send, recv_sem=recv, device_id=device, device_id_type=MESH
        )

    loads = [
        pltpu.make_async_copy(q_in, qbuf.at[me], lsem.at[0]),
        pltpu.make_async_copy(iq_in, iqbuf.at[mh], lsem.at[1]),
        pltpu.make_async_copy(w_in, wbuf.at[mh], lsem.at[2]),
        pltpu.make_async_copy(ik_in, ikbuf, lsem.at[3]),
        pltpu.make_async_copy(k_in, kbuf, lsem.at[4]),
    ]
    for load in loads:
        load.start()
    barrier = pltpu.get_barrier_semaphore()
    for i in range(1, N):
        pl.semaphore_signal(barrier, inc=1, device_id={"tokens": lax.rem(me + i, N)}, device_id_type=MESH)
    for i in range(1, NH):
        pl.semaphore_signal(barrier, inc=1, device_id={"heads": lax.rem(mh + i, NH)}, device_id_type=MESH)
    for load in loads[:3]:
        load.wait()
    pl.semaphore_wait(barrier, N - 1 + NH - 1)

    sends = []

    def go(copy):
        copy.start()
        sends.append(copy)

    def send_query(src, sem, dest):
        go(remote(qbuf.at[src], qbuf.at[src], sem, qr.at[src], tok=dest))

    def await_query(src):
        remote(qbuf.at[src], qbuf.at[src], zs.at[0], qr.at[src], tok=partner).wait_recv()

    for i in range(1, Z):
        send_query(me, zs.at[i], at(swapped(z, i, Z), y, core))
    for j in range(1, Y):
        send_query(me, ys.at[j], at(z, swapped(y, j, Y), core))
    send_query(me, cs.at[0], partner)
    for i in range(1, NH):
        other = lax.rem(mh + i, NH)
        go(remote(iqbuf.at[mh], iqbuf.at[mh], hs.at[i], hr.at[mh], head=other))
        go(remote(wbuf.at[mh], wbuf.at[mh], ws.at[i], wr.at[mh], head=other))

    key_index = me * Kl + lax.broadcasted_iota(jnp.int32, (1, Kl), 1)
    iscale = 128.0 ** (-0.5)

    def index_part(h):
        wt = jnp.transpose(wbuf[h])
        for t in range(Q):
            wcol[h, t * Jl : (t + 1) * Jl, :] = jnp.broadcast_to(wt[:, t : t + 1], (Jl, 128))
        act[h] = (
            lax.dot_general(iqbuf[h], ikbuf[...], (((1,), (1,)), ((), ())), preferred_element_type=f32) * iscale
        )

    def index_logits(h, first):
        def body(o, carry):
            parts = [[] for _ in range(Kl // 128)]
            for u in range(8):
                rows = pl.ds(pl.multiple_of((o * 8 + u) * Jl, 8), Jl)
                wc = wcol[h, rows, :]
                for lt in range(Kl // 128):
                    a = jnp.maximum(act[h, rows, lt * 128 : (lt + 1) * 128], 0.0)
                    parts[lt].append(jnp.sum(a * wc, axis=0, keepdims=True))
            eight = pl.ds(pl.multiple_of(o * 8, 8), 8)
            for lt in range(Kl // 128):
                lanes = slice(lt * 128, (lt + 1) * 128)
                part = jnp.concatenate(parts[lt], axis=0)
                ml[eight, lanes] = part if first else ml[eight, lanes] + part
            return carry

        lax.fori_loop(0, Q // 8, body, 0)

    eye128 = eye_of(128)

    def score_group(zg):
        group = qbuf[pl.ds(zg * G, G)].reshape(G * R, D)
        base = zg * (G * R)
        scores = lax.dot_general(group, kbuf[...], (((1,), (1,)), ((), ())), preferred_element_type=f32)
        step = min(32, R)
        for i in range(G):
            cap = jnp.where(key_index <= pos_ref[zg * G + i], open_value, masked_value)
            for r in range(0, R, step):
                row = i * R + r
                s = jnp.minimum(scores[row : row + step] * softmax_scale, cap)
                m = jnp.max(s, axis=1, keepdims=True)
                e = jnp.exp(s - m)
                p[pl.ds(pl.multiple_of(base + row, 8), step), :] = e
                colm[row : row + step, :] = m
                coll[row : row + step, :] = m + jnp.log(jnp.sum(e, axis=1, keepdims=True))
        for b in range(G * R // 128):
            mrow[zg, b : b + 1, :] = as_row(colm[b * 128 : (b + 1) * 128, :], eye128)
            stats[me, zg, b : b + 1, :] = as_row(coll[b * 128 : (b + 1) * 128, :], eye128)

    loads[3].wait()
    for i in range(NH):
        h = lax.rem(mh + i, NH)
        if i > 0:
            remote(iqbuf.at[h], iqbuf.at[h], hs.at[0], hr.at[h], head=lax.rem(mh + 1, NH)).wait_recv()
            remote(wbuf.at[h], wbuf.at[h], ws.at[0], wr.at[h], head=lax.rem(mh + 1, NH)).wait_recv()
        index_part(h)
        index_logits(h, i == 0)
        if i == 0:
            loads[4].wait()
            for j in range(1, Y):
                src = at(z, swapped(y, j, Y), core)
                await_query(src)
                send_query(src, cs.at[j], partner)
            for j in range(Y):
                await_query(at(z, swapped(y, j, Y), 1 - core))

    cap = jnp.concatenate([jnp.where(key_index <= pos_ref[t], open_value, masked_value) for t in range(Q)], axis=0)
    logits = jnp.minimum(ml[...], cap)
    ml[...] = logits
    imax = jnp.max(logits, axis=1, keepdims=True)
    isum = jnp.sum(jnp.exp(logits - imax), axis=1, keepdims=True)
    eyeq = eye_of(Q)
    istats[me, 0:1, :] = as_row(imax, eyeq)
    istats[me, 1:2, :] = as_row(isum, eyeq)
    for i in range(1, N):
        dst = lax.rem(me + i, N)
        go(remote(istats.at[me], istats.at[me], iss.at[i], isr.at[me], tok=dst))

    for i in range(1, Z):
        zz = swapped(z, i, Z)
        src = at(zz, y, core)
        await_query(src)
        for j in range(1, Y):
            send_query(src, ys.at[i * Y + j], at(z, swapped(y, j, Y), core))
        send_query(src, cs.at[i * Y], partner)
        score_group(swapped(z, i - 1, Z))
        for j in range(1, Y):
            src = at(zz, swapped(y, j, Y), core)
            await_query(src)
            send_query(src, cs.at[i * Y + j], partner)
        for j in range(Y):
            await_query(at(zz, swapped(y, j, Y), 1 - core))
    score_group(swapped(z, Z - 1, Z))

    for i in range(1, N):
        dst = lax.rem(me + i, N)
        go(remote(stats.at[me], stats.at[me], ss.at[i], sr.at[me], tok=dst))
    for i in range(1, N):
        src = lax.rem(me + i, N)
        remote(istats.at[src], istats.at[src], iss.at[0], isr.at[src], tok=partner).wait_recv()
    gmax = functools.reduce(jnp.maximum, [istats[i, 0:1, :] for i in range(N)])
    gsum = functools.reduce(jnp.add, [istats[i, 1:2, :] * jnp.exp(istats[i, 0:1, :] - gmax) for i in range(N)])
    gmax_col = jnp.sum(jnp.where(eyeq, gmax, 0.0), axis=1, keepdims=True)
    gsum_col = jnp.sum(jnp.where(eyeq, gsum, 0.0), axis=1, keepdims=True)
    dbuf[...] = jnp.exp(ml[...] - gmax_col) / gsum_col
    for i in range(1, N):
        src = lax.rem(me + i, N)
        remote(stats.at[src], stats.at[src], ss.at[0], sr.at[src], tok=partner).wait_recv()
    smax = functools.reduce(jnp.maximum, [stats[i] for i in range(N)])
    ssum = functools.reduce(jnp.add, [jnp.exp(stats[i] - smax) for i in range(N)])
    factor = jnp.exp(mrow[...] - smax) / ssum
    per = 128 // R
    for b in range(N * R // 128):
        bz, bb = divmod(b, G * R // 128)
        spread = jnp.transpose(jnp.broadcast_to(factor[bz][bb : bb + 1, :], (128, 128)))
        for u in range(per):
            t = b * per + u
            for lt in range(Kl // 128):
                lanes = slice(lt * 128, (lt + 1) * 128)
                tbuf[mh, t : t + 1, lanes] = jnp.sum(
                    p[t * R : (t + 1) * R, lanes] * spread[u * R : (u + 1) * R, :], axis=0, keepdims=True
                )
    for i in range(1, NH):
        go(remote(tbuf.at[mh], tbuf.at[mh], ts.at[i], tr.at[mh], head=lax.rem(mh + i, NH)))
    for i in range(1, NH):
        h = lax.rem(mh + i, NH)
        remote(tbuf.at[h], tbuf.at[h], ts.at[0], tr.at[h], head=lax.rem(mh + 1, NH)).wait_recv()
    target = functools.reduce(jnp.add, [tbuf[h] for h in range(NH)]) / H
    dbuf[...] = loss_scale * (dbuf[...] - target)

    def gates(h, own):
        eyej = eye_of(Jl)

        def body(t, carry):
            rows = pl.ds(pl.multiple_of(t * Jl, 8), Jl)
            d = dbuf[pl.ds(t, 1), :]
            wc = wcol[h, rows, :]
            total = jnp.zeros((Jl, 128), f32)
            for lt in range(Kl // 128):
                lanes = slice(lt * 128, (lt + 1) * 128)
                a = act[h, rows, lanes]
                dl = d[:, lanes]
                gate[h, rows, lanes] = jnp.where(a > 0.0, dl * wc, 0.0).astype(bf16)
                if own:
                    total = total + dl * jnp.maximum(a, 0.0)
            if own:
                row = as_row(jnp.sum(total, axis=1, keepdims=True), eyej)
                qpart[lax.rem(t, 2), lax.div(t, 2), Jl : Jl + 8, :] = jnp.broadcast_to(row, (8, 128))
            return carry

        lax.fori_loop(0, Q, body, 0, unroll=4)

    gates(mh, True)
    grads = jnp.dot(gate[mh], ikbuf[...], preferred_element_type=f32) * iscale
    for t in range(Q):
        qpart[t % 2, t // 2, 0:Jl, :] = grads[t * Jl : (t + 1) * Jl]
    pair = remote(qpart.at[1 - core], pairbuf, ps.at[0], pr.at[0], tok=partner)
    go(pair)
    for i in range(1, NH):
        gates(lax.rem(mh + i, NH), False)
    pair.wait_recv()
    rsend[...] = qpart[core] + pairbuf[...]
    for i in range(1, NC):
        other = lax.rem(chip + i, NC)
        go(remote(rsend.at[other], rsbuf.at[chip], rs.at[i], rr.at[chip], tok=other * 2 + core))
    total = jnp.zeros((128, Kl), f32)
    for h in range(NH):
        total = total + lax.dot_general(iqbuf[h], gate[h], (((0,), (0,)), ((), ())), preferred_element_type=f32)
    kg_out[...] = jnp.transpose(total)
    own = rsend[chip]
    for i in range(1, NC):
        src = lax.rem(chip + i, NC)
        remote(rsbuf.at[src], rsbuf.at[src], rs.at[0], rr.at[src], tok=partner).wait_recv()
        own = own + rsbuf[src]
    agbuf[me] = own.astype(bf16)
    for i in range(1, N):
        go(remote(agbuf.at[me], agbuf.at[me], gs.at[i], gr.at[me], tok=lax.rem(me + i, N)))
    for i in range(1, N):
        src = lax.rem(me + i, N)
        remote(agbuf.at[src], agbuf.at[src], gs.at[0], gr.at[src], tok=partner).wait_recv()
    qg_out[...] = agbuf[...]
    for copy in sends:
        copy.wait_send()


def local(queries, latent_keys, index_queries, index_keys, index_weights, positions):
    Hl, _, D = queries.shape
    Kl = latent_keys.shape[0]
    Q, Jl, DI = index_queries.shape
    N = lax.axis_size("tokens")
    NH = lax.axis_size("heads")
    chips = N // 2
    Z = 4 if chips % 4 == 0 else 1
    Y = chips // Z
    R = Hl
    SL = -(-(Jl + 8) // 8) * 8
    loss_scale = float(Kl * N // 8)
    cfg = (NH, N, Z, Y, Q, R, D, Kl, Jl, SL, float(Hl * NH), loss_scale)
    G = 2 * Y
    DMA = pltpu.SemaphoreType.DMA
    any_space = pl.BlockSpec(memory_space=pl.ANY)
    vmem = pl.BlockSpec(memory_space=pltpu.VMEM)
    slabs, keys = pl.pallas_call(
        functools.partial(kernel, cfg),
        out_shape=(
            jax.ShapeDtypeStruct((N, SL, 128), bf16),
            jax.ShapeDtypeStruct((Kl, 128), f32),
        ),
        in_specs=[any_space] * 5 + [pl.BlockSpec(memory_space=pltpu.SMEM)],
        out_specs=(vmem, vmem),
        scratch_shapes=[
            pltpu.VMEM((N, R, D), bf16),
            pltpu.VMEM((Kl, D), bf16),
            pltpu.VMEM((NH, Q * Jl, DI), bf16),
            pltpu.VMEM((Kl, DI), bf16),
            pltpu.VMEM((NH, Q, Jl), f32),
            pltpu.VMEM((NH, Q * Jl, 128), f32),
            pltpu.VMEM((N * R, Kl), f32),
            pltpu.VMEM((NH, Q * Jl, Kl), f32),
            pltpu.VMEM((NH, Q * Jl, Kl), bf16),
            pltpu.VMEM((Q, Kl), f32),
            pltpu.VMEM((Z, G * R // 128, 128), f32),
            pltpu.VMEM((G * R, 1), f32),
            pltpu.VMEM((G * R, 1), f32),
            pltpu.VMEM((N, Z, G * R // 128, 128), f32),
            pltpu.VMEM((N, 8, 128), f32),
            pltpu.VMEM((NH, Q, Kl), f32),
            pltpu.VMEM((Q, Kl), f32),
            pltpu.VMEM((2, chips, SL, 128), f32),
            pltpu.VMEM((chips, SL, 128), f32),
            pltpu.VMEM((chips, SL, 128), f32),
            pltpu.VMEM((chips, SL, 128), f32),
            pltpu.VMEM((N, SL, 128), bf16),
            DMA((5,)),
            DMA((Z,)),
            DMA((Z * Y,)),
            DMA((Z * Y,)),
            DMA((N,)),
            DMA((NH,)),
            DMA((NH,)),
            DMA((NH,)),
            DMA((NH,)),
            DMA((N,)),
            DMA((N,)),
            DMA((N,)),
            DMA((N,)),
            DMA((NH,)),
            DMA((NH,)),
            DMA((1,)),
            DMA((1,)),
            DMA((chips,)),
            DMA((chips,)),
            DMA((N,)),
            DMA((N,)),
        ],
        compiler_params=pltpu.CompilerParams(
            collective_id=0, has_side_effects=True, vmem_limit_bytes=60 * 1024 * 1024
        ),
    )(
        queries.reshape(Hl, D),
        latent_keys,
        index_queries.reshape(Q * Jl, DI),
        index_keys,
        index_weights,
        positions,
    )
    query_grad = slabs[:, :Jl, :].astype(f32)
    weight_grad = slabs[:, Jl, :Jl].astype(f32)
    return (query_grad, weight_grad, keys * (DI ** (-0.5)))


def solution(mesh):
    placed = (
        P("heads", "tokens", None),
        P("tokens", None),
        P(None, "heads", None),
        P("tokens", None),
        P(None, "heads"),
        P(),
    )
    return jax.shard_map(
        local,
        mesh=mesh,
        in_specs=placed,
        out_specs=(P(None, "heads", None), P(None, "heads"), P("tokens", None)),
        check_vma=False,
    )
```

time: 294 us -> 60.1 us (0.20)
  waiting for transfers between devices: 146 us -> 0 us
  blocking collectives: 101 us -> 0 us
  Pallas kernels: 0 us -> 51.8 us
  matrix products: 15.3 us -> 0 us
  between operations: 14.6 us -> 0.64 us
  local copies, waits for them, and re-layouts: 9.76 us -> 2.42 us
    psum x3 -> x0, waiting for transfers between devices: 105 us -> none  [the longest x1 53.7 us: local(): query_grad, weight_grad = lax.psum((query_local, weight_local), 'tokens')]
    pallas_call x0 -> x1, Pallas kernels: none -> 51.8 us  [local(): pl.pallas_call(functools.partial(kernel, cfg), out_shape=(jax.ShapeDtypeS...]
    all_gather x1 -> x0, waiting for transfers between devices: 39.6 us -> none  [local(): gathered = lax.all_gather(queries, 'tokens', axis=1, tiled=True)]
    all_gather x2 -> x0, blocking collectives: 38 us -> none  [merged(): everything = jax.tree.map(lambda part: lax.all_gather(part, axis), value)]
    unnamed x1 -> x0, blocking collectives: 32.6 us -> none
    psum x1 -> x0, blocking collectives: 30.6 us -> none  [local(): query_grad, weight_grad = lax.psum((query_local, weight_local), 'tokens')]
    dot_general x7 -> x0, matrix products: 15.3 us -> none  [the longest x4 10.6 us: block_scores(): jnp.einsum('hqd,kd->hqk', head_block, latent_keys, preferred_element_type...]
    unnamed x18 -> x1, local copies, waits for them, and re-layouts: 8.99 us -> 2.42 us
  transfers between devices with their start and end apart: 4 -> 0, of which waited for: 4 -> 0; matrix products, arithmetic and copies ran while one was open for 2% -> 0% of each run, Pallas kernels for 0% -> 0%
where the time goes in v1:
time: 60.1 us; the launch traced here: 59.8 us
  Pallas kernels  51.8 us (86%)
  other arithmetic  4.87 us (8%)
  local copies, waits for them, and re-layouts  2.42 us (4%)
  between operations  0.64 us (1%)
    pallas_call x1, Pallas kernels, local(): pl.pallas_call(functools.partial(kernel, cfg), out_shape=(jax.ShapeDtypeS...  51.8 us
    unnamed x1, local copies, waits for them, and re-layouts  2.42 us
    mul x1, other arithmetic, local(): return (query_grad, weight_grad, keys * DI ** (-0.5))  1.88 us
    convert_element_type x1, other arithmetic, local(): query_grad = slabs[:, :Jl, :].astype(f32)  1.63 us
    convert_element_type x1, other arithmetic, local(): weight_grad = slabs[:, Jl, :Jl].astype(f32)  1.36 us

profile of v1, /device:TPU:0, one launch (start us, length us, event | category | flops | bytes accessed | tf_op | source)
XLA Modules:
  0.0 59.8 jit_solution(12370041901417532436)
XLA Ops:
  0.6 2.4 %copy.9.k_in = bf16[1024,576]{1,0:T(8,128)(2,1)} copy(bf16[1024,576]{0,1:T(8,128)(2,1)} %param.7) | data formatting | bytes 2359296 | tf_op args[1]
  3.1 51.8 %shard_map.85 = (bf16[16,40,128]{2,1,0:T(8,128)(2,1)}, f32[1024,128]{1,0:T(8,128)}) custom-call(bf16[64,576]{1,0:T(8,128)(2,1)} %bitcast.4, bf16[1024,576]{1,0:T(8,128)(2,1)} %copy.9.k_in, bf16[512,128]{1,0:T(8,128)(2,1)} %bitcast.3, bf16[1024,128]{1,0:T(8,128)(2,1)} %ik_in.1, f32[16,32]{1,0:T(8,128)} %w_in.1, s32[16]{0:T(128)} %pos_ref.1), custom_call_target="tpu_custom_call" | custom-call | tf_op jit(solution)/shard_map/pallas_call | solution.py:307
  54.9 1.9 %broadcast_multiply_fusion = f32[1024,128]{1,0:T(8,128)} fusion(f32[1024,128]{1,0:T(8,128)} %get-tuple-element.6), kind=kLoop, calls=%fused_computation | loop fusion | flops 131072 | bytes 1048576 | tf_op jit(solution)/shard_map/mul | solution.py:373
  56.8 1.4 %slice_convert_fusion.1 = f32[16,1,32]{2,1,0:T(1,128)} fusion(bf16[16,40,128]{2,1,0:T(8,128)(2,1)} %get-tuple-element.5), kind=kLoop, calls=%fused_computation.2 | loop fusion | flops 512 | bytes 3072 | tf_op jit(solution)/shard_map/convert_element_type | solution.py:372
  58.1 1.6 %slice_convert_fusion = f32[16,32,128]{2,1,0:T(8,128)} fusion(bf16[16,40,128]{2,1,0:T(8,128)(2,1)} %get-tuple-element.5), kind=kLoop, calls=%fused_computation.1 | loop fusion | flops 65536 | bytes 393216 | tf_op jit(solution)/shard_map/convert_element_type | solution.py:371

commit v2 on v1

--- a/solution.py
+++ b/solution.py
@@ -54,6 +54,9 @@
 
     def at(zz, yy, cc):
         return (zz * Y + yy) * 2 + cc
+
+    def peer(i):
+        return at(swapped(z, i // G, Z), swapped(y, i // 2 % Y, Y), swapped(core, i % 2, 2))
 
     def remote(src, dst, send, recv, tok=None, head=None):
         device = {"tokens": tok} if head is None else {"heads": head}
@@ -135,7 +138,7 @@
     def score_group(zg):
         group = qbuf[pl.ds(zg * G, G)].reshape(G * R, D)
         base = zg * (G * R)
-        scores = lax.dot_general(group, kbuf[...], (((1,), (1,)), ((), ())), preferred_element_type=f32)
+        scores = lax.dot_general(group, kbuf[...], (((1,), (0,)), ((), ())), preferred_element_type=f32)
         step = min(32, R)
         for i in range(G):
             cap = jnp.where(key_index <= pos_ref[zg * G + i], open_value, masked_value)
@@ -151,54 +154,80 @@
             mrow[zg, b : b + 1, :] = as_row(colm[b * 128 : (b + 1) * 128, :], eye128)
             stats[me, zg, b : b + 1, :] = as_row(coll[b * 128 : (b + 1) * 128, :], eye128)
 
-    loads[3].wait()
-    for i in range(NH):
-        h = lax.rem(mh + i, NH)
-        if i > 0:
-            remote(iqbuf.at[h], iqbuf.at[h], hs.at[0], hr.at[h], head=lax.rem(mh + 1, NH)).wait_recv()
-            remote(wbuf.at[h], wbuf.at[h], ws.at[0], wr.at[h], head=lax.rem(mh + 1, NH)).wait_recv()
-        index_part(h)
-        index_logits(h, i == 0)
-        if i == 0:
-            loads[4].wait()
-            for j in range(1, Y):
-                src = at(z, swapped(y, j, Y), core)
-                await_query(src)
-                send_query(src, cs.at[j], partner)
-            for j in range(Y):
-                await_query(at(z, swapped(y, j, Y), 1 - core))
-
-    cap = jnp.concatenate([jnp.where(key_index <= pos_ref[t], open_value, masked_value) for t in range(Q)], axis=0)
-    logits = jnp.minimum(ml[...], cap)
-    ml[...] = logits
-    imax = jnp.max(logits, axis=1, keepdims=True)
-    isum = jnp.sum(jnp.exp(logits - imax), axis=1, keepdims=True)
-    eyeq = eye_of(Q)
-    istats[me, 0:1, :] = as_row(imax, eyeq)
-    istats[me, 1:2, :] = as_row(isum, eyeq)
-    for i in range(1, N):
-        dst = lax.rem(me + i, N)
-        go(remote(istats.at[me], istats.at[me], iss.at[i], isr.at[me], tok=dst))
-
-    for i in range(1, Z):
-        zz = swapped(z, i, Z)
-        src = at(zz, y, core)
+    def await_index(h):
+        other = lax.rem(mh + 1, NH)
+        remote(iqbuf.at[h], iqbuf.at[h], hs.at[0], hr.at[h], head=other).wait_recv()
+        remote(wbuf.at[h], wbuf.at[h], ws.at[0], wr.at[h], head=other).wait_recv()
+
+    def index_stats():
+        cap = jnp.concatenate(
+            [jnp.where(key_index <= pos_ref[t], open_value, masked_value) for t in range(Q)], axis=0
+        )
+        logits = jnp.minimum(ml[...], cap)
+        ml[...] = logits
+        imax = jnp.max(logits, axis=1, keepdims=True)
+        isum = jnp.sum(jnp.exp(logits - imax), axis=1, keepdims=True)
+        istats[me, 0:1, :] = as_row(imax, eyeq)
+        istats[me, 1:2, :] = as_row(isum, eyeq)
+        for i in range(1, N):
+            dst = lax.rem(me + i, N)
+            go(remote(istats.at[me], istats.at[me], iss.at[i], isr.at[me], tok=dst))
+
+    def relay_z(i):
+        src = at(swapped(z, i, Z), y, core)
         await_query(src)
         for j in range(1, Y):
             send_query(src, ys.at[i * Y + j], at(z, swapped(y, j, Y), core))
         send_query(src, cs.at[i * Y], partner)
-        score_group(swapped(z, i - 1, Z))
+
+    def relay_y(i):
         for j in range(1, Y):
-            src = at(zz, swapped(y, j, Y), core)
+            src = at(swapped(z, i, Z), swapped(y, j, Y), core)
             await_query(src)
             send_query(src, cs.at[i * Y + j], partner)
+
+    def await_pair(i):
         for j in range(Y):
-            await_query(at(zz, swapped(y, j, Y), 1 - core))
-    score_group(swapped(z, Z - 1, Z))
+            await_query(at(swapped(z, i, Z), swapped(y, j, Y), 1 - core))
+
+    def index_rest():
+        for i in range(1, NH):
+            h = lax.rem(mh + i, NH)
+            await_index(h)
+            index_part(h)
+            index_logits(h, False)
+        index_stats()
+
+    eyeq = eye_of(Q)
+    loads[3].wait()
+    index_part(mh)
+    index_logits(mh, True)
+    relay_y(0)
+    loads[4].wait()
+    for i in range(1, Z):
+        relay_z(i)
+        if i == 1:
+            await_pair(0)
+            score_group(z)
+        else:
+            relay_y(i - 1)
+    index_rest()
+    if Z == 1:
+        await_pair(0)
+        score_group(z)
+    else:
+        for i in range(1, Z - 1):
+            await_pair(i)
+            if i == Z - 2:
+                relay_y(Z - 1)
+            score_group(swapped(z, i, Z))
+        if Z == 2:
+            relay_y(1)
+        await_pair(Z - 1)
+        score_group(swapped(z, Z - 1, Z))
 
     for i in range(1, N):
-        dst = lax.rem(me + i, N)
-        go(remote(stats.at[me], stats.at[me], ss.at[i], sr.at[me], tok=dst))
+        go(remote(stats.at[me], stats.at[me], ss.at[i], sr.at[me], tok=peer(N - i)))
     for i in range(1, N):
         src = lax.rem(me + i, N)
         remote(istats.at[src], istats.at[src], iss.at[0], isr.at[src], tok=partner).wait_recv()
@@ -264,8 +293,8 @@
         gates(lax.rem(mh + i, NH), False)
     pair.wait_recv()
     rsend[...] = qpart[core] + pairbuf[...]
-    for i in range(1, NC):
-        other = lax.rem(chip + i, NC)
+    for i in range(NC - 1, 0, -1):
+        other = lax.div(peer(2 * i), 2)
         go(remote(rsend.at[other], rsbuf.at[chip], rs.at[i], rr.at[chip], tok=other * 2 + core))
     total = jnp.zeros((128, Kl), f32)
     for h in range(NH):
@@ -277,14 +306,21 @@
         remote(rsbuf.at[src], rsbuf.at[src], rs.at[0], rr.at[src], tok=partner).wait_recv()
         own = own + rsbuf[src]
     agbuf[me] = own.astype(bf16)
-    for i in range(1, N):
-        go(remote(agbuf.at[me], agbuf.at[me], gs.at[i], gr.at[me], tok=lax.rem(me + i, N)))
+    for i in range(N - 1, 0, -1):
+        go(remote(agbuf.at[me], agbuf.at[me], gs.at[i], gr.at[me], tok=peer(i)))
     for i in range(1, N):
         src = lax.rem(me + i, N)
         remote(agbuf.at[src], agbuf.at[src], gs.at[0], gr.at[src], tok=partner).wait_recv()
     qg_out[...] = agbuf[...]
     for copy in sends:
         copy.wait_send()
+
+
+def finish(Jl, scale, slabs, keys, query_grad, weight_grad, key_grad):
+    key_grad[...] = keys[...] * scale
+    query_grad[...] = slabs[:, 0:Jl, :].astype(f32)
+    for t in range(slabs.shape[0]):
+        weight_grad[t : t + 1, :] = slabs[t, Jl : Jl + 8, 0:Jl].astype(f32)[0:1]
 
 
 def local(queries, latent_keys, index_queries, index_keys, index_weights, positions):
@@ -314,7 +350,7 @@
         out_specs=(vmem, vmem),
         scratch_shapes=[
             pltpu.VMEM((N, R, D), bf16),
-            pltpu.VMEM((Kl, D), bf16),
+            pltpu.VMEM((D, Kl), bf16),
             pltpu.VMEM((NH, Q * Jl, DI), bf16),
             pltpu.VMEM((Kl, DI), bf16),
             pltpu.VMEM((NH, Q, Jl), f32),
@@ -327,7 +363,7 @@
             pltpu.VMEM((G * R, 1), f32),
             pltpu.VMEM((G * R, 1), f32),
             pltpu.VMEM((N, Z, G * R // 128, 128), f32),
-            pltpu.VMEM((N, 8, 128), f32),
+            pltpu.VMEM((N, 2, 128), f32),
             pltpu.VMEM((NH, Q, Kl), f32),
             pltpu.VMEM((Q, Kl), f32),
             pltpu.VMEM((2, chips, SL, 128), f32),
@@ -362,15 +398,22 @@
         ),
     )(
         queries.reshape(Hl, D),
-        latent_keys,
+        latent_keys.T,
         index_queries.reshape(Q * Jl, DI),
         index_keys,
         index_weights,
         positions,
     )
-    query_grad = slabs[:, :Jl, :].astype(f32)
-    weight_grad = slabs[:, Jl, :Jl].astype(f32)
-    return (query_grad, weight_grad, keys * (DI ** (-0.5)))
+    return pl.pallas_call(
+        functools.partial(finish, Jl, DI ** (-0.5)),
+        out_shape=(
+            jax.ShapeDtypeStruct((Q, Jl, DI), f32),
+            jax.ShapeDtypeStruct((Q, Jl), f32),
+            jax.ShapeDtypeStruct((Kl, DI), f32),
+        ),
+        in_specs=[vmem, vmem],
+        out_specs=(vmem, vmem, vmem),
+    )(slabs, keys)
 
 
 def solution(mesh):

time: 60.1 us -> 48.9 us (0.81)
  other arithmetic: 4.87 us -> 0 us
  Pallas kernels: 51.8 us -> 48.1 us
  local copies, waits for them, and re-layouts: 2.42 us -> 0 us
    pallas_call x1, Pallas kernels: 51.8 us -> 46 us  [local(): pl.pallas_call(functools.partial(kernel, cfg), out_shape=(jax.ShapeDtypeS...]
    convert_element_type x2 -> x0, other arithmetic: 2.99 us -> none  [the longest x1 1.63 us: local(): query_grad = slabs[:, :Jl, :].astype(f32)]
    unnamed x1 -> x0, local copies, waits for them, and re-layouts: 2.42 us -> none
    pallas_call x0 -> x1, Pallas kernels: none -> 2.06 us  [local(): pl.pallas_call(functools.partial(finish, Jl, DI ** (-0.5)), out_shape=(ja...]
    mul x1 -> x0, other arithmetic: 1.88 us -> none  [local(): return (query_grad, weight_grad, keys * DI ** (-0.5))]
where the time goes in v2:
time: 48.9 us; the launch traced here: 48.7 us
  Pallas kernels  48.1 us (98%)
  between operations  0.64 us (1%)
    pallas_call x1, Pallas kernels, local(): pl.pallas_call(functools.partial(kernel, cfg), out_shape=(jax.ShapeDtypeS...  46 us
    pallas_call x1, Pallas kernels, local(): pl.pallas_call(functools.partial(finish, Jl, DI ** (-0.5)), out_shape=(ja...  2.06 us

profile of v2, /device:TPU:0, one launch (start us, length us, event | category | flops | bytes accessed | tf_op | source)
XLA Modules:
  0.0 48.7 jit_solution(1185416868355285276)
XLA Ops:
  0.6 46.0 %shard_map.85 = (bf16[16,40,128]{2,1,0:T(8,128)(2,1)}, f32[1024,128]{1,0:T(8,128)}) custom-call(bf16[64,576]{1,0:T(8,128)(2,1)} %bitcast.5, bf16[576,1024]{1,0:T(8,128)(2,1)} %bitcast.3, bf16[512,128]{1,0:T(8,128)(2,1)} %bitcast.4, bf16[1024,128]{1,0:T(8,128)(2,1)} %ik_in.1, f32[16,32]{1,0:T(8,128)} %w_in.1, s32[16]{0:T(128)} %pos_ref.1), custom_call_target="tpu_custom_call" | custom-call | tf_op jit(solution)/shard_map/pallas_call | solution.py:343
  46.7 2.1 %shard_map.86 = (f32[16,32,128]{2,1,0:T(8,128)}, f32[16,32]{1,0:T(8,128)}, f32[1024,128]{1,0:T(8,128)}) custom-call(bf16[16,40,128]{2,1,0:T(8,128)(2,1)} %get-tuple-element.5.slabs, f32[1024,128]{1,0:T(8,128)} %get-tuple-element.6.keys), custom_call_target="tpu_custom_call" | custom-call | tf_op jit(solution)/shard_map/pallas_call | solution.py:407

commit v3 on v2

--- a/solution.py
+++ b/solution.py
@@ -190,39 +190,44 @@
         for j in range(Y):
             await_query(at(swapped(z, i, Z), swapped(y, j, Y), 1 - core))
 
-    def index_rest():
-        for i in range(1, NH):
-            h = lax.rem(mh + i, NH)
-            await_index(h)
-            index_part(h)
-            index_logits(h, False)
-        index_stats()
-
     eyeq = eye_of(Q)
     loads[3].wait()
     index_part(mh)
     index_logits(mh, True)
     relay_y(0)
     loads[4].wait()
+    others = [lax.rem(mh + i, NH) for i in range(1, NH)]
+
+    def other_parts():
+        for h in others:
+            await_index(h)
+            index_part(h)
+
+    def other_logits():
+        for h in others:
+            index_logits(h, False)
+        index_stats()
+
+    if Z == 1:
+        other_parts()
+        other_logits()
+        await_pair(0)
+        score_group(z)
     for i in range(1, Z):
         relay_z(i)
         if i == 1:
             await_pair(0)
             score_group(z)
+        elif i == 2:
+            other_parts()
+    for i in range(1, Z):
+        relay_y(i)
+        if i == 1:
+            other_logits()
         else:
-            relay_y(i - 1)
-    index_rest()
-    if Z == 1:
-        await_pair(0)
-        score_group(z)
-    else:
-        for i in range(1, Z - 1):
-            await_pair(i)
-            if i == Z - 2:
-                relay_y(Z - 1)
-            score_group(swapped(z, i, Z))
-        if Z == 2:
-            relay_y(1)
+            await_pair(i - 1)
+            score_group(swapped(z, i - 1, Z))
+    if Z > 1:
         await_pair(Z - 1)
         score_group(swapped(z, Z - 1, Z))
 
@@ -243,25 +248,28 @@
     ssum = functools.reduce(jnp.add, [jnp.exp(stats[i] - smax) for i in range(N)])
     factor = jnp.exp(mrow[...] - smax) / ssum
     per = 128 // R
-    for b in range(N * R // 128):
-        bz, bb = divmod(b, G * R // 128)
-        spread = jnp.transpose(jnp.broadcast_to(factor[bz][bb : bb + 1, :], (128, 128)))
-        for u in range(per):
-            t = b * per + u
-            for lt in range(Kl // 128):
-                lanes = slice(lt * 128, (lt + 1) * 128)
-                tbuf[mh, t : t + 1, lanes] = jnp.sum(
-                    p[t * R : (t + 1) * R, lanes] * spread[u * R : (u + 1) * R, :], axis=0, keepdims=True
-                )
-    for i in range(1, NH):
-        go(remote(tbuf.at[mh], tbuf.at[mh], ts.at[i], tr.at[mh], head=lax.rem(mh + i, NH)))
-    for i in range(1, NH):
-        h = lax.rem(mh + i, NH)
-        remote(tbuf.at[h], tbuf.at[h], ts.at[0], tr.at[h], head=lax.rem(mh + 1, NH)).wait_recv()
-    target = functools.reduce(jnp.add, [tbuf[h] for h in range(NH)]) / H
-    dbuf[...] = loss_scale * (dbuf[...] - target)
-
-    def gates(h, own):
+    parts = 2 if Q % 16 == 0 else 1
+    QP = Q // parts
+
+    def rows_of(part):
+        return pl.ds(part * QP, QP)
+
+    for part in range(parts):
+        for b in range(part * QP // per, (part + 1) * QP // per):
+            bz, bb = divmod(b, G * R // 128)
+            spread = jnp.transpose(jnp.broadcast_to(factor[bz][bb : bb + 1, :], (128, 128)))
+            for u in range(per):
+                t = b * per + u
+                for lt in range(Kl // 128):
+                    lanes = slice(lt * 128, (lt + 1) * 128)
+                    tbuf[mh, t : t + 1, lanes] = jnp.sum(
+                        p[t * R : (t + 1) * R, lanes] * spread[u * R : (u + 1) * R, :], axis=0, keepdims=True
+                    )
+        for i in range(1, NH):
+            block = tbuf.at[mh, rows_of(part)]
+            go(remote(block, block, ts.at[part, i], tr.at[part, mh], head=lax.rem(mh + i, NH)))
+
+    def gates(h, own, first, last):
         eyej = eye_of(Jl)
 
         def body(t, carry):
@@ -281,17 +289,33 @@
                 qpart[lax.rem(t, 2), lax.div(t, 2), Jl : Jl + 8, :] = jnp.broadcast_to(row, (8, 128))
             return carry
 
-        lax.fori_loop(0, Q, body, 0, unroll=4)
-
-    gates(mh, True)
-    grads = jnp.dot(gate[mh], ikbuf[...], preferred_element_type=f32) * iscale
-    for t in range(Q):
-        qpart[t % 2, t // 2, 0:Jl, :] = grads[t * Jl : (t + 1) * Jl]
-    pair = remote(qpart.at[1 - core], pairbuf, ps.at[0], pr.at[0], tok=partner)
-    go(pair)
-    for i in range(1, NH):
-        gates(lax.rem(mh + i, NH), False)
-    pair.wait_recv()
+        lax.fori_loop(first, last, body, 0, unroll=4)
+
+    pairs = []
+    for part in range(parts):
+        for h in others:
+            block = tbuf.at[h, rows_of(part)]
+            remote(block, block, ts.at[part, 0], tr.at[part, h], head=others[0]).wait_recv()
+        rows = slice(part * QP, (part + 1) * QP)
+        target = functools.reduce(jnp.add, [tbuf[h, rows, :] for h in range(NH)]) / H
+        dbuf[rows, :] = loss_scale * (dbuf[rows, :] - target)
+        gates(mh, True, part * QP, (part + 1) * QP)
+        grads = (
+            jnp.dot(gate[mh, part * QP * Jl : (part + 1) * QP * Jl, :], ikbuf[...], preferred_element_type=f32)
+            * iscale
+        )
+        for i in range(QP):
+            t = part * QP + i
+            qpart[t % 2, t // 2, 0:Jl, :] = grads[i * Jl : (i + 1) * Jl]
+        span = pl.ds(part * QP // 2, QP // 2)
+        pairs.append(
+            remote(qpart.at[1 - core, span], pairbuf.at[span], ps.at[part], pr.at[part], tok=partner)
+        )
+        go(pairs[-1])
+    for h in others:
+        gates(h, False, 0, Q)
+    for pair in pairs:
+        pair.wait_recv()
     rsend[...] = qpart[core] + pairbuf[...]
     for i in range(NC - 1, 0, -1):
         other = lax.div(peer(2 * i), 2)
@@ -306,11 +330,19 @@
         remote(rsbuf.at[src], rsbuf.at[src], rs.at[0], rr.at[src], tok=partner).wait_recv()
         own = own + rsbuf[src]
     agbuf[me] = own.astype(bf16)
-    for i in range(N - 1, 0, -1):
-        go(remote(agbuf.at[me], agbuf.at[me], gs.at[i], gr.at[me], tok=peer(i)))
-    for i in range(1, N):
-        src = lax.rem(me + i, N)
+    for i in range(NC - 1, 0, -1):
+        go(remote(agbuf.at[me], agbuf.at[me], gs.at[2 * i], gr.at[me], tok=peer(2 * i)))
+    go(remote(agbuf.at[me], agbuf.at[me], gs.at[1], gr.at[me], tok=partner))
+
+    def await_slab(src):
         remote(agbuf.at[src], agbuf.at[src], gs.at[0], gr.at[src], tok=partner).wait_recv()
+
+    for i in range(1, NC):
+        src = peer(2 * i)
+        await_slab(src)
+        go(remote(agbuf.at[src], agbuf.at[src], gs.at[2 * i + 1], gr.at[src], tok=partner))
+    for i in range(NC):
+        await_slab(peer(2 * i + 1))
     qg_out[...] = agbuf[...]
     for copy in sends:
         copy.wait_send()
@@ -384,10 +416,10 @@
             DMA((N,)),
             DMA((N,)),
             DMA((N,)),
-            DMA((NH,)),
-            DMA((NH,)),
-            DMA((1,)),
-            DMA((1,)),
+            DMA((2, NH)),
+            DMA((2, NH)),
+            DMA((2,)),
+            DMA((2,)),
             DMA((chips,)),
             DMA((chips,)),
             DMA((N,)),

time: 48.9 us -> 46.4 us (0.949)
  Pallas kernels: 48.1 us -> 45.6 us
    pallas_call x1, Pallas kernels: 46 us -> 43.5 us  [local(): pl.pallas_call(functools.partial(kernel, cfg), out_shape=(jax.ShapeDtypeS...]
where the time goes in v3:
time: 46.4 us; the launch traced here: 46.2 us
  Pallas kernels  45.6 us (98%)
  between operations  0.64 us (1%)
    pallas_call x1, Pallas kernels, local(): pl.pallas_call(functools.partial(kernel, cfg), out_shape=(jax.ShapeDtypeS...  43.5 us
    pallas_call x1, Pallas kernels, local(): pl.pallas_call(functools.partial(finish, Jl, DI ** (-0.5)), out_shape=(ja...  2.06 us

profile of v3, /device:TPU:0, one launch (start us, length us, event | category | flops | bytes accessed | tf_op | source)
XLA Modules:
  0.0 46.2 jit_solution(1638724059711355504)
XLA Ops:
  0.6 43.5 %shard_map.85 = (bf16[16,40,128]{2,1,0:T(8,128)(2,1)}, f32[1024,128]{1,0:T(8,128)}) custom-call(bf16[64,576]{1,0:T(8,128)(2,1)} %bitcast.5, bf16[576,1024]{1,0:T(8,128)(2,1)} %bitcast.3, bf16[512,128]{1,0:T(8,128)(2,1)} %bitcast.4, bf16[1024,128]{1,0:T(8,128)(2,1)} %ik_in.1, f32[16,32]{1,0:T(8,128)} %w_in.1, s32[16]{0:T(128)} %pos_ref.1), custom_call_target="tpu_custom_call" | custom-call | tf_op jit(solution)/shard_map/pallas_call | solution.py:375
  44.2 2.1 %shard_map.86 = (f32[16,32,128]{2,1,0:T(8,128)}, f32[16,32]{1,0:T(8,128)}, f32[1024,128]{1,0:T(8,128)}) custom-call(bf16[16,40,128]{2,1,0:T(8,128)(2,1)} %get-tuple-element.5.slabs, f32[1024,128]{1,0:T(8,128)} %get-tuple-element.6.keys), custom_call_target="tpu_custom_call" | custom-call | tf_op jit(solution)/shard_map/pallas_call | solution.py:439
